TPU v7x, 512 devices: a whole 4x4x16 slice. The times are simulated.
512 devices in a mesh: seq: 128 (over x_lo, y, z), mp: 4 (over x_hi, core).
Axes of the slice: x: 4 (x_hi: 2, x_lo: 2; x = x_hi * 2 + x_lo), y: 4, z: 16, core: 2. Of those that a mesh axis runs over, the one named last changes fastest.
Arguments:
- incoming_image_patches: bfloat16 [1, 128, 128, 1152], P(None, 'seq', 'mp'), may hold values from -6 to 6
- initial_standardize_scaling: float32 [1152], replicated, may hold values from 0.1 to 1.9
- acceptance_matrix: bfloat16 [1152, 1024], P(None, 'mp'), may hold values from -0.1875 to 0.1875
- addressing_matrix: bfloat16 [1152, 1024], P(None, 'mp'), may hold values from -0.1875 to 0.1875
- content_matrix: bfloat16 [1152, 1024], P(None, 'mp'), may hold values from -0.1875 to 0.1875
- forgetting_lowdim_left_factor: bfloat16 [1152, 64], replicated, may hold values from -0.1875 to 0.1875
- forgetting_lowdim_right_factor: bfloat16 [64, 1024], P(None, 'mp'), may hold values from -1.5 to 1.5
- forgetting_baseline: float32 [1024], P('mp'), may hold values from -6 to 1
- self_token_reward: float32 [1024], P('mp'), may hold values from -3 to 3
- horizontal_cluster_scaling: float32 [1024], P('mp'), may hold values from 0.1 to 1.9
- vertical_cluster_scaling: float32 [1024], P('mp'), may hold values from 0.1 to 1.9
- temporal_mix_projection_matrix: bfloat16 [1024, 1152], P('mp'), may hold values from -0.1875 to 0.1875
- later_standardize_scaling: float32 [1152], replicated, may hold values from 0.1 to 1.9
- feature_mix_addressing_matrix: bfloat16 [1152, 4608], P('seq', 'mp'), may hold values from -0.1875 to 0.1875
- feature_mix_content_matrix: bfloat16 [4608, 1152], P('mp', 'seq'), may hold values from -0.09375 to 0.09375
Outputs:
- block_out: bfloat16 [1, 128, 128, 1152], P(None, 'seq', 'mp')
All inputs are finite; a program needn't handle non-finite values.
Results may differ from a plain program's by a relative error of at most 0.017.
Values may be sent and summed in bfloat16 or wider, within the bound.
No kernel may reach another device: no remote copies, remote signals or barrier semaphores. Data moves between devices by JAX's collectives and lax.ppermute only.
A program may use at most 64 MiB of HBM per device.

v0:
```python
import jax
import jax.numpy as jnp
from jax import lax
from jax.sharding import Mesh
from jax.sharding import PartitionSpec as P

SUBSPACE_SIZE = 64
SEQ = ("x_lo", "y", "z")
MP = ("x_hi", "core")
PLANE = ("x_lo", "y")


def from_everyone(value, axis):
    copies = jnp.broadcast_to(value, (lax.axis_size(axis), *value.shape))
    return lax.all_to_all(copies, axis, split_axis=0, concat_axis=0, tiled=True)


def split_up(value, dim, size):
    lengths = value.shape
    pieces = value.reshape(*lengths[:dim], size, lengths[dim] // size, *lengths[dim + 1 :])
    return jnp.moveaxis(pieces, dim, 0)


def sent_and_summed(value, axis, dim):
    size = lax.axis_size(axis)
    pieces = lax.all_to_all(split_up(value, dim, size), axis, 0, 0, tiled=True)
    return jnp.sum(pieces.astype(jnp.float32), axis=0)


def layer_norm(inputs, gain):
    values = inputs.astype(jnp.float32)
    average = jnp.mean(values, axis=-1, keepdims=True)
    centred = values - average
    spread = jnp.mean(centred * centred, axis=-1, keepdims=True)
    return (centred * lax.rsqrt(spread + 1e-05) * gain).astype(jnp.bfloat16)


def heads_first(array, nheads):
    number, length, inner_width = array.shape
    shaped = array.astype(jnp.float32).reshape(number, length, nheads, inner_width // nheads)
    return shaped.transpose(0, 2, 1, 3)


def recurrence(recept_in, keying_in, decays_in, valued_in, boost_in, gain):
    number, length, inner_width = recept_in.shape
    nheads = inner_width // SUBSPACE_SIZE
    head_size = inner_width // nheads
    blocks = length // 16
    acceptance_horizontal_lines = heads_first(recept_in, nheads)
    addressing_horizontal_lines = heads_first(keying_in, nheads)
    decays = heads_first(decays_in, nheads)
    content_horizontal_lines = heads_first(valued_in, nheads)
    boost = boost_in.reshape(nheads, 1, head_size)
    running = jnp.cumsum(decays, axis=2)
    before = running - decays
    before_blocks = before.reshape(number, nheads, blocks, 16, head_size)
    anchor = before_blocks[:, :, :, :1, :]
    queries = acceptance_horizontal_lines.reshape(number, nheads, blocks, 16, head_size) * jnp.exp(
        before_blocks - anchor
    )
    places = jnp.arange(length)
    limits = (jnp.arange(blocks) + 1) * 16
    usable = places[None, :] < limits[:, None]
    exponent = anchor - running[:, :, None, :, :]
    exponent = jnp.where(usable[None, None, :, :, None], exponent, -10000.0)
    weighted = addressing_horizontal_lines[:, :, None, :, :] * jnp.exp(exponent)
    scores = jnp.einsum("nhbqc,nhbsc->nhbqs", queries, weighted, precision=lax.Precision.HIGHEST)
    query_places = places.reshape(blocks, 16)
    earlier = places[None, None, :] < query_places[:, :, None]
    scores = jnp.where(earlier[None, None], scores, 0.0)
    current = jnp.sum(acceptance_horizontal_lines * boost * addressing_horizontal_lines, axis=-1)
    summed = jnp.einsum(
        "nhbqs,nhsc->nhbqc", scores, content_horizontal_lines, precision=lax.Precision.HIGHEST
    )
    summed = (
        summed.reshape(number, nheads, length, head_size)
        + current[..., None] * content_horizontal_lines
    )
    average = jnp.mean(summed, axis=-1, keepdims=True)
    centred = summed - average
    spread = jnp.mean(centred * centred, axis=-1, keepdims=True)
    normed = (
        (centred * lax.rsqrt(spread + 0.00064))
        .transpose(0, 2, 1, 3)
        .reshape(number, length, inner_width)
    )
    return (normed * gain).astype(jnp.bfloat16)


def unit_order(planes, depth, width):
    stored = jnp.arange(planes * depth * width)
    z, rest = (stored // (planes * width), stored % (planes * width))
    plane, row = (rest // width, rest % width)
    true_place = (plane * depth + z) * width + row
    return true_place


def shards(
    incoming_image_patches,
    initial_standardize_scaling,
    acceptance_matrix,
    addressing_matrix,
    content_matrix,
    forgetting_lowdim_left_factor,
    forgetting_lowdim_right_factor,
    forgetting_baseline,
    self_token_reward,
    horizontal_cluster_scaling,
    vertical_cluster_scaling,
    temporal_mix_projection_matrix,
    later_standardize_scaling,
    feature_mix_addressing_matrix,
    feature_mix_content_matrix,
):
    images, row_count, part_cols, model_width = incoming_image_patches.shape
    tokens = incoming_image_patches.reshape(part_cols, model_width)
    whole_rows = lax.all_gather(tokens, MP, axis=0, tiled=True)
    full_cols = whole_rows.shape[0]
    inner_width = acceptance_matrix.shape[1]
    planes, depth = (lax.axis_size(PLANE), lax.axis_size("z"))
    width = feature_mix_addressing_matrix.shape[0]
    pair = jnp.stack([feature_mix_addressing_matrix, feature_mix_content_matrix.T])
    plane_pair = from_everyone(pair, PLANE).reshape(planes, *pair.shape)
    plane_up = plane_pair[:, 0].reshape(planes * width, -1)
    plane_down = plane_pair[:, 1].reshape(planes * width, -1)
    full_up = lax.all_gather(plane_up, "z", axis=0, tiled=True)
    full_down = lax.all_gather(plane_down, "z", axis=0, tiled=True)
    xn1 = layer_norm(whole_rows, initial_standardize_scaling)
    recept = jnp.dot(xn1, acceptance_matrix, preferred_element_type=jnp.float32).astype(
        jnp.bfloat16
    )
    keying = jnp.dot(xn1, addressing_matrix, preferred_element_type=jnp.float32).astype(
        jnp.bfloat16
    )
    valued = jnp.dot(xn1, content_matrix, preferred_element_type=jnp.float32).astype(jnp.bfloat16)
    latent = jnp.tanh(
        jnp.dot(xn1, forgetting_lowdim_left_factor, preferred_element_type=jnp.float32)
    ).astype(jnp.bfloat16)
    decay = (
        -0.7
        * jax.nn.sigmoid(
            forgetting_baseline
            + jnp.dot(latent, forgetting_lowdim_right_factor, preferred_element_type=jnp.float32)
        )
    ).astype(jnp.bfloat16)
    row_out = recurrence(
        recept[None],
        keying[None],
        decay[None],
        valued[None],
        self_token_reward,
        horizontal_cluster_scaling,
    )[0]
    sent = jnp.stack([recept, keying, decay, row_out], axis=1)
    got = lax.all_to_all(
        sent.reshape(full_cols, 4 * inner_width // 128, 128),
        SEQ,
        split_axis=0,
        concat_axis=0,
        tiled=True,
    )
    height = got.shape[0]
    got = got.reshape(height, 4, inner_width)
    col_out = recurrence(
        got[None, :, 0],
        got[None, :, 1],
        got[None, :, 2],
        got[None, :, 3],
        self_token_reward,
        vertical_cluster_scaling,
    )[0]
    back = lax.all_to_all(
        col_out.reshape(height, inner_width // 128, 128),
        SEQ,
        split_axis=0,
        concat_axis=0,
        tiled=True,
    ).reshape(full_cols, inner_width)
    partial_value = jnp.dot(
        back, temporal_mix_projection_matrix, preferred_element_type=jnp.float32
    ).astype(jnp.bfloat16)
    attended = sent_and_summed(partial_value, MP, 0)
    residual = (tokens.astype(jnp.float32) + attended).astype(jnp.bfloat16)
    mix_input = layer_norm(residual, later_standardize_scaling)
    places = unit_order(planes, depth, width)
    moved = (jnp.arange(model_width)[:, None] == places[None, :]).astype(jnp.bfloat16)
    mix_input = jnp.dot(mix_input, moved, preferred_element_type=jnp.float32).astype(jnp.bfloat16)
    mix_all = lax.all_gather(mix_input, MP, axis=0, tiled=True)
    hidden_pre = jnp.dot(mix_all, full_up, preferred_element_type=jnp.float32)
    positive = jnp.maximum(hidden_pre, 0.0)
    hidden = (positive * positive).astype(jnp.bfloat16)
    downward = lax.dot_general(
        hidden, full_down, (((1,), (1,)), ((), ())), preferred_element_type=jnp.float32
    ).astype(jnp.bfloat16)
    downward = lax.dot_general(
        downward, moved, (((1,), (1,)), ((), ())), preferred_element_type=jnp.float32
    ).astype(jnp.bfloat16)
    mixed = sent_and_summed(downward, MP, 0)
    block_out = (residual.astype(jnp.float32) + mixed).astype(jnp.bfloat16)
    return block_out.reshape(images, row_count, part_cols, model_width)


def solution(mesh):
    torus = Mesh(mesh.devices.reshape(2, 4, 16, 2, 2), (*SEQ, *MP))
    return jax.shard_map(
        shards,
        mesh=torus,
        in_specs=(
            P(None, SEQ, MP, None),
            P(),
            P(None, MP),
            P(None, MP),
            P(None, MP),
            P(),
            P(None, MP),
            P(MP),
            P(MP),
            P(MP),
            P(MP),
            P(MP, None),
            P(),
            P(SEQ, MP),
            P(MP, SEQ),
        ),
        out_specs=P(None, SEQ, MP, None),
        check_vma=False,
    )
```

profile of v0, /device:TPU:1, one launch (start us, length us, event | category | flops | bytes accessed | tf_op | source)
XLA Modules:
  0.0 206.6 jit_solution(17887059847881086414)
XLA Ops:
  6.6 0.0 all-gather.4.cloned.1.call-start
  6.6 0.9 pad_maximum_fusion.1
  7.5 0.2 broadcast_in_dim.42
  7.7 12.3 %all_to_all.25 = bf16[8,2,9,1152]{3,1,2,0:T(2,128)(2,1)S(1)} all-to-all(bf16[8,2,9,1152]{3,1,2,0:T(2,128)(2,1)S(1)} %broadcast_in_dim.42), channel_id=1, replica_groups=mesh['x_lo'=2,'y'=4,'z'=16,'x_hi'=2,'core'=2] {'x_lo','y'}, dimensions={0} | all-to-all | bytes 663552 | tf_op jit(solution)/shard_map/all_to_all | solution.py:15
  20.1 1.5 slice_reduce_fusion
  21.6 0.0 copy-start.5
  21.6 0.7 reshape_squeeze.7
  22.3 0.0 all-gather.4.cloned.1.call-update
  22.4 11.8 %all-gather = bf16[1,1,128,1152]{3,2,1,0:T(8,128)(2,1)S(1)} all-gather(bf16[1,1,32,1152]{3,2,1,0:T(8,128)(2,1)S(1)} %copy-done.1), channel_id=2, replica_groups=mesh['x_lo'=2,'y'=4,'z'=16,'x_hi'=2,'core'=2] {'x_hi','core'}, dimensions={2}, use_global_device_ids=true | all-gather | bytes 368640 | tf_op jit(solution)/shard_map/all_gather | solution.py:117
  34.2 0.1 convert_reduce_fusion
  34.3 0.2 fusion.26
  34.6 0.0 copy-start.6
  34.6 0.5 fusion.13
  35.2 0.1 copy.93
  35.3 0.1 copy.94
  35.4 0.3 reduce_window_sum.17
  35.7 0.1 copy.96
  35.9 0.3 convolution_convert_fusion.4
  36.2 0.1 copy.91
  36.3 0.1 copy.92
  36.4 0.0 copy-start.4
  36.4 0.3 convolution_convert_fusion.3
  36.8 0.1 copy.95
  36.9 1.4 convolution_convert_fusion.2
  38.3 0.1 copy.97
  38.4 0.1 iota_compare_fusion.8
  38.5 0.1 iota_compare_fusion.7
  38.6 1.2 convolution_select_fusion.1
  39.8 0.2 fusion.94
  40.1 0.1 copy.98
  40.2 0.1 mul.219
  40.3 0.1 multiply_reduce_fusion.2
  40.5 0.1 copy.99
  40.7 0.2 copy.100
  40.9 0.9 copy.101
  41.8 15.7 %all-to-all-start = ((bf16[128,8,128]{2,1,0:T(8,128)(2,1)}), bf16[128,8,128]{2,1,0:T(8,128)(2,1)S(1)}, u32[]{:S(2)}, u32[]{:S(2)}) async-start(bf16[128,8,128]{2,1,0:T(8,128)(2,1)} %copy.101), calls=%async_computation | async-start | bytes 524288 | tf_op jit(solution)/shard_map/all_to_all | solution.py:155
  57.5 0.0 all-gather.6.cloned.1.call-start
  57.5 0.8 reshape_squeeze.8
  58.3 0.0 all-gather.6.cloned.1.call-update
  58.3 22.2 %all-to-all-done = bf16[128,8,128]{2,1,0:T(8,128)(2,1)S(1)} async-done(((bf16[128,8,128]{2,1,0:T(8,128)(2,1)}), bf16[128,8,128]{2,1,0:T(8,128)(2,1)S(1)}, u32[]{:S(2)}, u32[]{:S(2)}) %all-to-all-start) | async-done | bytes 262176 | tf_op jit(solution)/shard_map/all_to_all | solution.py:155
  80.5 0.2 copy.102
  80.8 0.1 copy.104
  80.9 0.3 reduce_window_sum.18
  81.2 0.1 copy.105
  81.3 0.1 copy.103
  81.5 1.2 convolution_select_fusion
  82.7 0.2 fusion.95
  83.0 0.1 copy.106
  83.1 0.1 fusion.55
  83.4 0.1 copy.107
  83.5 0.1 copy.108
  83.6 22.7 %all_to_all.26 = bf16[128,2,128]{2,1,0:T(2,128)(2,1)S(1)} all-to-all(bf16[128,2,128]{2,1,0:T(2,128)(2,1)S(1)} %copy.108), channel_id=1, replica_groups=mesh['x_lo'=2,'y'=4,'z'=16,'x_hi'=2,'core'=2] {'x_lo','y','z'}, dimensions={0} | all-to-all | bytes 131072 | tf_op jit(solution)/shard_map/all_to_all | solution.py:172
  106.3 1.0 convolution_convert_fusion.1
  107.2 7.1 %all-to-all-start.2 = ((bf16[4,32,1152]{2,1,0:T(8,128)(2,1)}), bf16[4,32,1152]{2,1,0:T(8,128)(2,1)S(1)}, u32[]{:S(2)}, u32[]{:S(2)}) async-start(bf16[4,32,1152]{2,1,0:T(8,128)(2,1)} %bitcast.53), calls=%async_computation.2 | async-start | bytes 589824 | tf_op jit(solution)/shard_map/all_to_all | solution.py:26
  114.3 6.9 %all-to-all-done.2 = bf16[4,32,1152]{2,1,0:T(8,128)(2,1)S(1)} async-done(((bf16[4,32,1152]{2,1,0:T(8,128)(2,1)}), bf16[4,32,1152]{2,1,0:T(8,128)(2,1)S(1)}, u32[]{:S(2)}, u32[]{:S(2)}) %all-to-all-start.2) | async-done | bytes 294944 | tf_op jit(solution)/shard_map/all_to_all | solution.py:26
  121.2 0.1 convert_reduce_fusion.3
  121.4 0.2 fusion.47
  121.6 1.1 fusion.7
  122.7 8.2 %all_gather.13 = bf16[128,1152]{1,0:T(8,128)(2,1)S(1)} all-gather(bf16[32,1152]{1,0:T(8,128)(2,1)S(1)} %fusion.7), channel_id=1, replica_groups=mesh['x_lo'=2,'y'=4,'z'=16,'x_hi'=2,'core'=2] {'x_hi','core'}, dimensions={0}, use_global_device_ids=true | all-gather | bytes 368640 | tf_op jit(solution)/shard_map/all_gather | solution.py:188
  130.9 2.4 %fusion.5 = bf16[128,1152]{1,0:T(8,128)(2,1)S(1)} fusion(bf16[128,1152]{1,0:T(8,128)(2,1)S(1)} %all_gather.13, bf16[1152,1152]{1,0:T(8,128)(2,1)} %all-gather.4.cloned.1.call-done), kind=kOutput, calls=%fused_computation.7 | convolution fusion | flops 340180992 | bytes 3244032 | tf_op jit(solution)/shard_map/dot_general | solution.py:189
  133.3 40.7 %all-gather.6.cloned.1.call-done = bf16[1152,1152]{1,0:T(8,128)(2,1)} async-done(((bf16[72,1152]{1,0:T(8,128)(2,1)}), bf16[1152,1152]{1,0:T(8,128)(2,1)}) %all-gather.6.cloned.1.call-update) | async-done | bytes 2654224 | tf_op jit(solution)/shard_map/all_gather | solution.py:127
  174.0 3.7 %fusion.6 = bf16[128,1152]{1,0:T(8,128)(2,1)S(1)} fusion(s32[1152]{0:T(1024)S(1)} %fusion.74, bf16[128,1152]{1,0:T(8,128)(2,1)S(1)} %fusion.5, bf16[1152,1152]{1,0:T(8,128)(2,1)} %all-gather.6.cloned.1.call-done), kind=kOutput, calls=%fused_computation.8 | convolution fusion | flops 681099264 | bytes 3248640 | tf_op jit(solution)/shard_map/dot_general | solution.py:195
  177.6 21.4 %all_to_all.27 = bf16[4,32,1152]{2,1,0:T(8,128)(2,1)S(1)} all-to-all(bf16[4,32,1152]{2,1,0:T(8,128)(2,1)S(1)} %bitcast.162), channel_id=1, replica_groups=mesh['x_lo'=2,'y'=4,'z'=16,'x_hi'=2,'core'=2] {'x_hi','core'}, dimensions={0} | all-to-all | bytes 589824 | tf_op jit(solution)/shard_map/all_to_all | solution.py:26
  199.1 0.7 fusion.53
  (50 shorter events, 0.7 us)
Async XLA Ops:
  6.5 99.7 %copy-start = (bf16[256,1152]{1,0:T(8,128)(2,1)S(1)}, bf16[256,1152]{1,0:T(8,128)(2,1)}, u32[]{:S(2)}) copy-start(bf16[256,1152]{1,0:T(8,128)(2,1)} %param.26) | copy-start | bytes 1769476
  6.5 15.8 %copy-start.1 = (bf16[1,1,32,1152]{3,2,1,0:T(8,128)(2,1)S(1)}, bf16[1,1,32,1152]{3,2,1,0:T(8,128)(2,1)}, u32[]{:S(2)}) copy-start(bf16[1,1,32,1152]{3,2,1,0:T(8,128)(2,1)} %param.15) | copy-start | bytes 221188
  6.5 28.0 %copy-start.9 = (f32[1152]{0:T(1024)S(1)}, f32[1152]{0:T(1024)}, u32[]{:S(2)}) copy-start(f32[1152]{0:T(1024)} %param.16) | copy-start | bytes 13828
  6.5 28.0 %copy-start.7 = (bf16[1152,64]{0,1:T(8,128)(2,1)S(1)}, bf16[1152,64]{0,1:T(8,128)(2,1)}, u32[]{:S(2)}) copy-start(bf16[1152,64]{0,1:T(8,128)(2,1)} %param.20) | copy-start | bytes 442372
  6.5 28.1 %copy-start.8 = (bf16[64,256]{1,0:T(8,128)(2,1)S(1)}, bf16[64,256]{1,0:T(8,128)(2,1)}, u32[]{:S(2)}) copy-start(bf16[64,256]{1,0:T(8,128)(2,1)} %param.21) | copy-start | bytes 98308
  6.5 28.1 %copy-start.11 = (f32[256]{0:T(256)S(1)}, f32[256]{0:T(256)}, u32[]{:S(2)}) copy-start(f32[256]{0:T(256)} %param.22) | copy-start | bytes 3076
  6.6 124.3 %all-gather.4.cloned.1.call-start = ((), (), s32[]{:S(2)}) async-start(), calls=%async_computation.5 | async-start | bytes 2820096 | tf_op jit(solution)/shard_map/all_gather | solution.py:126
  21.6 14.3 %copy-start.5 = (bf16[1152,256]{1,0:T(8,128)(2,1)S(1)}, bf16[1152,256]{1,0:T(8,128)(2,1)}, u32[]{:S(2)}) copy-start(bf16[1152,256]{1,0:T(8,128)(2,1)} %param.17) | copy-start | bytes 1769476
  34.6 1.8 copy-start.6
  36.4 3.7 %copy-start.4 = (f32[256]{0:T(256)S(1)}, f32[256]{0:T(256)}, u32[]{:S(2)}) copy-start(f32[256]{0:T(256)} %param.23) | copy-start | bytes 3076
  36.9 3.8 %copy-start.2 = (f32[256]{0:T(256)S(1)}, f32[256]{0:T(256)}, u32[]{:S(2)}) copy-start(f32[256]{0:T(256)} %param.24) | copy-start | bytes 3076
  41.8 38.7 %all-to-all-start = ((bf16[128,8,128]{2,1,0:T(8,128)(2,1)}), bf16[128,8,128]{2,1,0:T(8,128)(2,1)S(1)}, u32[]{:S(2)}, u32[]{:S(2)}) async-start(bf16[128,8,128]{2,1,0:T(8,128)(2,1)} %copy.101), calls=%async_computation | async-start | bytes 524288 | tf_op jit(solution)/shard_map/all_to_all | solution.py:155
  57.5 116.5 %all-gather.6.cloned.1.call-start = ((), (), s32[]{:S(2)}) async-start(), calls=%async_computation.6 | async-start | bytes 2820096 | tf_op jit(solution)/shard_map/all_gather | solution.py:127
  81.2 2.3 %copy-start.3 = (f32[256]{0:T(256)S(1)}, f32[256]{0:T(256)}, u32[]{:S(2)}) copy-start(f32[256]{0:T(256)} %param.25) | copy-start | bytes 3076
  82.7 38.9 %copy-start.10 = (f32[1152]{0:T(1024)S(1)}, f32[1152]{0:T(1024)}, u32[]{:S(2)}) copy-start(f32[1152]{0:T(1024)} %param.27) | copy-start | bytes 13828
  107.2 14.0 %all-to-all-start.2 = ((bf16[4,32,1152]{2,1,0:T(8,128)(2,1)}), bf16[4,32,1152]{2,1,0:T(8,128)(2,1)S(1)}, u32[]{:S(2)}, u32[]{:S(2)}) async-start(bf16[4,32,1152]{2,1,0:T(8,128)(2,1)} %bitcast.53), calls=%async_computation.2 | async-start | bytes 589824 | tf_op jit(solution)/shard_map/all_to_all | solution.py:26
Sparse Core Ops, SparseCore 0:
  22.5 78.9 all-gather.3
  103.5 70.3 all-gather.5
where the time goes:
time: 207 us
  blocking collectives  76.4 us (37%)
  waiting for transfers between devices  69.8 us (34%)
  starting transfers between devices  22.8 us (11%)
  between operations  13.9 us (7%)
  matrix products  13.6 us (7%)
  local copies, waits for them, and re-layouts  6.29 us (3%)
  other arithmetic  3.71 us (2%)
    all_gather x1, waiting for transfers between devices, shards(): full_down = lax.all_gather(plane_down, 'z', axis=0, tiled=True)  40.7 us
    all_to_all x1, blocking collectives, shards(): lax.all_to_all(col_out.reshape(height, inner_width // 128, 128), SEQ, spl...  22.7 us
    all_to_all x1, waiting for transfers between devices, shards(): lax.all_to_all(sent.reshape(full_cols, 4 * inner_width // 128, 128), SEQ,...  22.2 us
    all_to_all x1, blocking collectives, sent_and_summed(): pieces = lax.all_to_all(split_up(value, dim, size), axis, 0, 0, tiled=True)  21.4 us
    all_to_all x1, starting transfers between devices, shards(): lax.all_to_all(sent.reshape(full_cols, 4 * inner_width // 128, 128), SEQ,...  15.7 us
    all_to_all x1, blocking collectives, from_everyone(): return lax.all_to_all(copies, axis, split_axis=0, concat_axis=0, tiled=True)  12.3 us
    all_gather x1, blocking collectives, shards(): whole_rows = lax.all_gather(tokens, MP, axis=0, tiled=True)  11.8 us
    all_gather x1, blocking collectives, shards(): mix_all = lax.all_gather(mix_input, MP, axis=0, tiled=True)  8.17 us
  transfers between devices with their start and end apart: 4, of which 3 were waited for; matrix products, arithmetic and copies ran while one was open for 8% of the time, Pallas kernels for 0%

commit v1 on v0

--- a/solution.py
+++ b/solution.py
@@ -114,7 +114,9 @@
 ):
     images, row_count, part_cols, model_width = incoming_image_patches.shape
     tokens = incoming_image_patches.reshape(part_cols, model_width)
-    whole_rows = lax.all_gather(tokens, MP, axis=0, tiled=True)
+    whole_rows = jnp.concatenate(
+        lax.all_to_all(jnp.stack([tokens] * lax.axis_size(MP)), MP, 0, 0), axis=0
+    )
     full_cols = whole_rows.shape[0]
     inner_width = acceptance_matrix.shape[1]
     planes, depth = (lax.axis_size(PLANE), lax.axis_size("z"))

time: 207 us -> 215 us (1.039)
  blocking collectives: 76.4 us -> 51.4 us
  waiting for transfers between devices: 69.8 us -> 84 us
  starting transfers between devices: 22.8 us -> 36.3 us
  local copies, waits for them, and re-layouts: 6.29 us -> 11.2 us
    all_to_all x0 -> x2, starting transfers between devices: none -> 14.8 us  [the longest x1 8.84 us: shards(): lax.all_to_all(jnp.stack([tokens] * lax.axis_size(MP)), MP, 0, 0)]
    all_to_all x1 -> x0, blocking collectives: 12.3 us -> none  [from_everyone(): return lax.all_to_all(copies, axis, split_axis=0, concat_axis=0, tiled=True)]
    all_gather x1 -> x0, blocking collectives: 11.8 us -> none  [shards(): whole_rows = lax.all_gather(tokens, MP, axis=0, tiled=True)]
    all_to_all x0 -> x2, waiting for transfers between devices: none -> 10 us  [the longest x1 5.5 us: from_everyone(): return lax.all_to_all(copies, axis, split_axis=0, concat_axis=0, tiled=True)]
    all_gather x1, waiting for transfers between devices: 40.7 us -> 44.4 us  [shards(): full_down = lax.all_gather(plane_down, 'z', axis=0, tiled=True)]
  transfers between devices with their start and end apart: 4 -> 6, of which waited for: 3 -> 5; matrix products, arithmetic and copies ran while one was open for 8% -> 9% of each run, Pallas kernels for 0% -> 0%
where the time goes in v1:
time: 215 us; the launch traced here: 214 us
  waiting for transfers between devices  84 us (39%)
  blocking collectives  51.4 us (24%)
  starting transfers between devices  36.3 us (17%)
  between operations  14 us (7%)
  matrix products  13.2 us (6%)
  local copies, waits for them, and re-layouts  11.2 us (5%)
  other arithmetic  3.91 us (2%)
    all_gather x1, waiting for transfers between devices, shards(): full_down = lax.all_gather(plane_down, 'z', axis=0, tiled=True)  44.4 us
    all_to_all x1, waiting for transfers between devices, shards(): lax.all_to_all(sent.reshape(full_cols, 4 * inner_width // 128, 128), SEQ,...  22.7 us
    all_to_all x1, blocking collectives, shards(): lax.all_to_all(col_out.reshape(height, inner_width // 128, 128), SEQ, spl...  21.8 us
    all_to_all x1, blocking collectives, sent_and_summed(): pieces = lax.all_to_all(split_up(value, dim, size), axis, 0, 0, tiled=True)  21.4 us
    all_to_all x1, starting transfers between devices, shards(): lax.all_to_all(sent.reshape(full_cols, 4 * inner_width // 128, 128), SEQ,...  15.1 us
    all_to_all x1, starting transfers between devices, shards(): lax.all_to_all(jnp.stack([tokens] * lax.axis_size(MP)), MP, 0, 0)  8.84 us
    all_gather x1, blocking collectives, shards(): mix_all = lax.all_gather(mix_input, MP, axis=0, tiled=True)  8.17 us
    all_to_all x1, waiting for transfers between devices, sent_and_summed(): pieces = lax.all_to_all(split_up(value, dim, size), axis, 0, 0, tiled=True)  6.87 us
  transfers between devices with their start and end apart: 6, of which 5 were waited for; matrix products, arithmetic and copies ran while one was open for 9% of the time, Pallas kernels for 0%

profile of v1, /device:TPU:1, one launch (start us, length us, event | category | flops | bytes accessed | tf_op | source)
XLA Modules:
  0.0 213.9 jit_solution(10251653952551385043)
XLA Ops:
  6.5 0.9 pad_maximum_fusion.1
  7.5 0.9 broadcast_in_dim.42
  8.4 5.9 %all-to-all-start.4 = ((bf16[8,2,9,1152]{3,1,2,0:T(2,128)(2,1)}), bf16[8,2,9,1152]{3,1,2,0:T(2,128)(2,1)S(1)}, u32[]{:S(2)}, u32[]{:S(2)}) async-start(bf16[8,2,9,1152]{3,1,2,0:T(2,128)(2,1)} %broadcast_in_dim.42), calls=%async_computation.4 | async-start | bytes 663552 | tf_op jit(solution)/shard_map/all_to_all | solution.py:15
  14.3 0.8 mul.220
  15.1 0.1 iota_compare_fusion.7
  15.2 5.5 %all-to-all-done.4 = bf16[8,2,9,1152]{3,1,2,0:T(2,128)(2,1)S(1)} async-done(((bf16[8,2,9,1152]{3,1,2,0:T(2,128)(2,1)}), bf16[8,2,9,1152]{3,1,2,0:T(2,128)(2,1)S(1)}, u32[]{:S(2)}, u32[]{:S(2)}) %all-to-all-start.4) | async-done | bytes 331808 | tf_op jit(solution)/shard_map/all_to_all | solution.py:15
  20.7 1.6 stack.24
  22.3 8.8 %all-to-all-start = ((bf16[4,32,1152]{2,1,0:T(8,128)(2,1)}), bf16[4,32,1152]{2,1,0:T(8,128)(2,1)S(1)}, u32[]{:S(2)}, u32[]{:S(2)}) async-start(bf16[4,32,1152]{2,1,0:T(8,128)(2,1)} %stack.24), calls=%async_computation | async-start | bytes 589824 | tf_op jit(solution)/shard_map/all_to_all | solution.py:118
  31.1 1.5 slice_reduce_fusion
  32.7 0.7 reshape_squeeze.7
  33.4 0.1 iota_compare_fusion.8
  33.5 4.5 %all-to-all-done = bf16[4,32,1152]{2,1,0:T(8,128)(2,1)S(1)} async-done(((bf16[4,32,1152]{2,1,0:T(8,128)(2,1)}), bf16[4,32,1152]{2,1,0:T(8,128)(2,1)S(1)}, u32[]{:S(2)}, u32[]{:S(2)}) %all-to-all-start) | async-done | bytes 294944 | tf_op jit(solution)/shard_map/all_to_all | solution.py:118
  38.0 0.1 convert_reduce_fusion.2
  38.2 0.1 div.52
  38.2 0.2 multiply_reduce_fusion
  38.5 0.1 rsqrt.36
  38.6 0.2 fusion.25
  38.8 0.5 fusion.13
  39.3 0.1 copy.111
  39.4 0.1 copy.112
  39.6 0.4 copy-done.7
  39.9 0.3 reduce_window_sum.17
  40.2 0.7 copy-done.5
  41.0 0.8 copy.114
  41.7 0.3 convolution_convert_fusion.4
  42.0 0.1 copy.109
  42.1 0.1 copy.110
  42.3 0.3 convolution_convert_fusion.3
  42.5 0.1 copy.113
  42.7 0.3 convolution_convert_fusion.2
  42.9 0.1 copy.115
  43.0 2.1 convolution_select_fusion.1
  45.2 0.3 fusion.83
  45.4 0.1 copy.116
  45.6 0.1 multiply_reduce_fusion.3
  45.8 0.1 copy.117
  46.0 0.2 copy.118
  46.2 0.9 copy.119
  47.1 15.1 %all-to-all-start.1 = ((bf16[128,8,128]{2,1,0:T(8,128)(2,1)}), bf16[128,8,128]{2,1,0:T(8,128)(2,1)S(1)}, u32[]{:S(2)}, u32[]{:S(2)}) async-start(bf16[128,8,128]{2,1,0:T(8,128)(2,1)} %copy.119), calls=%async_computation.1 | async-start | bytes 524288 | tf_op jit(solution)/shard_map/all_to_all | solution.py:157
  62.2 0.8 reshape_squeeze.8
  63.0 22.7 %all-to-all-done.1 = bf16[128,8,128]{2,1,0:T(8,128)(2,1)S(1)} async-done(((bf16[128,8,128]{2,1,0:T(8,128)(2,1)}), bf16[128,8,128]{2,1,0:T(8,128)(2,1)S(1)}, u32[]{:S(2)}, u32[]{:S(2)}) %all-to-all-start.1) | async-done | bytes 262176 | tf_op jit(solution)/shard_map/all_to_all | solution.py:157
  85.7 0.2 copy.120
  86.0 0.1 copy.122
  86.1 0.3 reduce_window_sum.18
  86.5 0.1 copy.123
  86.6 0.1 copy.121
  86.7 1.2 convolution_select_fusion
  88.0 0.2 fusion.84
  88.2 0.1 copy.124
  88.3 0.1 fusion.50
  88.6 0.1 copy.125
  88.8 21.8 %all_to_all.30 = bf16[128,2,128]{2,1,0:T(2,128)(2,1)S(1)} all-to-all(bf16[128,2,128]{2,1,0:T(2,128)(2,1)S(1)} %copy.126), channel_id=1, replica_groups=mesh['x_lo'=2,'y'=4,'z'=16,'x_hi'=2,'core'=2] {'x_lo','y','z'}, dimensions={0} | all-to-all | bytes 131072 | tf_op jit(solution)/shard_map/all_to_all | solution.py:174
  110.6 1.0 convolution_convert_fusion.1
  111.6 6.4 %all-to-all-start.3 = ((bf16[4,32,1152]{2,1,0:T(8,128)(2,1)}), bf16[4,32,1152]{2,1,0:T(8,128)(2,1)S(1)}, u32[]{:S(2)}, u32[]{:S(2)}) async-start(bf16[4,32,1152]{2,1,0:T(8,128)(2,1)} %bitcast.54), calls=%async_computation.3 | async-start | bytes 589824 | tf_op jit(solution)/shard_map/all_to_all | solution.py:26
  118.0 6.9 %all-to-all-done.3 = bf16[4,32,1152]{2,1,0:T(8,128)(2,1)S(1)} async-done(((bf16[4,32,1152]{2,1,0:T(8,128)(2,1)}), bf16[4,32,1152]{2,1,0:T(8,128)(2,1)S(1)}, u32[]{:S(2)}, u32[]{:S(2)}) %all-to-all-start.3) | async-done | bytes 294944 | tf_op jit(solution)/shard_map/all_to_all | solution.py:26
  124.9 0.1 convert_reduce_fusion.3
  125.1 0.2 fusion.44
  125.3 1.1 fusion.7
  126.4 8.2 %all_gather.9 = bf16[128,1152]{1,0:T(8,128)(2,1)S(1)} all-gather(bf16[32,1152]{1,0:T(8,128)(2,1)S(1)} %fusion.7), channel_id=1, replica_groups=mesh['x_lo'=2,'y'=4,'z'=16,'x_hi'=2,'core'=2] {'x_hi','core'}, dimensions={0}, use_global_device_ids=true | all-gather | bytes 368640 | tf_op jit(solution)/shard_map/all_gather | solution.py:190
  134.6 2.4 %fusion.5 = bf16[128,1152]{1,0:T(8,128)(2,1)S(1)} fusion(bf16[128,1152]{1,0:T(8,128)(2,1)S(1)} %all_gather.9, bf16[1152,1152]{1,0:T(8,128)(2,1)} %all-gather.3.cloned.1.call-done), kind=kOutput, calls=%fused_computation.7 | convolution fusion | flops 340180992 | bytes 3244032 | tf_op jit(solution)/shard_map/dot_general | solution.py:191
  137.0 44.4 %all-gather.5.cloned.1.call-done = bf16[1152,1152]{1,0:T(8,128)(2,1)} async-done(((bf16[72,1152]{1,0:T(8,128)(2,1)}), bf16[1152,1152]{1,0:T(8,128)(2,1)}) %all-gather.5.cloned.1.call-update) | async-done | bytes 2654224 | tf_op jit(solution)/shard_map/all_gather | solution.py:129
  181.3 3.7 %fusion.6 = bf16[128,1152]{1,0:T(8,128)(2,1)S(1)} fusion(s32[1152]{0:T(1024)S(1)} %fusion.69, bf16[128,1152]{1,0:T(8,128)(2,1)S(1)} %fusion.5, bf16[1152,1152]{1,0:T(8,128)(2,1)} %all-gather.5.cloned.1.call-done), kind=kOutput, calls=%fused_computation.8 | convolution fusion | flops 681099264 | bytes 3248640 | tf_op jit(solution)/shard_map/dot_general | solution.py:197
  185.0 21.4 %all_to_all.31 = bf16[4,32,1152]{2,1,0:T(8,128)(2,1)S(1)} all-to-all(bf16[4,32,1152]{2,1,0:T(8,128)(2,1)S(1)} %bitcast.156), channel_id=1, replica_groups=mesh['x_lo'=2,'y'=4,'z'=16,'x_hi'=2,'core'=2] {'x_hi','core'}, dimensions={0} | all-to-all | bytes 589824 | tf_op jit(solution)/shard_map/all_to_all | solution.py:26
  206.4 0.7 fusion.47
  (64 shorter events, 0.8 us)
Async XLA Ops:
  6.5 104.1 %copy-start = (bf16[256,1152]{1,0:T(8,128)(2,1)S(1)}, bf16[256,1152]{1,0:T(8,128)(2,1)}, u32[]{:S(2)}) copy-start(bf16[256,1152]{1,0:T(8,128)(2,1)} %param.26) | copy-start | bytes 1769476
  6.5 32.0 %copy-start.9 = (f32[1152]{0:T(1024)S(1)}, f32[1152]{0:T(1024)}, u32[]{:S(2)}) copy-start(f32[1152]{0:T(1024)} %param.16) | copy-start | bytes 13828
  7.4 31.4 %copy-start.12 = (bf16[1152,64]{0,1:T(8,128)(2,1)S(1)}, bf16[1152,64]{0,1:T(8,128)(2,1)}, u32[]{:S(2)}) copy-start(bf16[1152,64]{0,1:T(8,128)(2,1)} %param.20) | copy-start | bytes 442372
  7.4 31.4 %copy-start.13 = (bf16[64,256]{1,0:T(8,128)(2,1)S(1)}, bf16[64,256]{1,0:T(8,128)(2,1)}, u32[]{:S(2)}) copy-start(bf16[64,256]{1,0:T(8,128)(2,1)} %param.21) | copy-start | bytes 98308
  7.4 31.4 %copy-start.15 = (f32[256]{0:T(256)S(1)}, f32[256]{0:T(256)}, u32[]{:S(2)}) copy-start(f32[256]{0:T(256)} %param.22) | copy-start | bytes 3076
  8.4 12.3 %all-to-all-start.4 = ((bf16[8,2,9,1152]{3,1,2,0:T(2,128)(2,1)}), bf16[8,2,9,1152]{3,1,2,0:T(2,128)(2,1)S(1)}, u32[]{:S(2)}, u32[]{:S(2)}) async-start(bf16[8,2,9,1152]{3,1,2,0:T(2,128)(2,1)} %broadcast_in_dim.42), calls=%async_computation.4 | async-start | bytes 663552 | tf_op jit(solution)/shard_map/all_to_all | solution.py:15
  22.3 15.7 %all-to-all-start = ((bf16[4,32,1152]{2,1,0:T(8,128)(2,1)}), bf16[4,32,1152]{2,1,0:T(8,128)(2,1)S(1)}, u32[]{:S(2)}, u32[]{:S(2)}) async-start(bf16[4,32,1152]{2,1,0:T(8,128)(2,1)} %stack.24), calls=%async_computation | async-start | bytes 589824 | tf_op jit(solution)/shard_map/all_to_all | solution.py:118
  31.1 103.5 %all-gather.3.cloned.1.call-start = ((), (), s32[]{:S(2)}) async-start(), calls=%async_computation.6 | async-start | bytes 2820096 | tf_op jit(solution)/shard_map/all_gather | solution.py:128
  32.6 9.1 %copy-start.2 = (bf16[1152,256]{1,0:T(8,128)(2,1)S(1)}, bf16[1152,256]{1,0:T(8,128)(2,1)}, u32[]{:S(2)}) copy-start(bf16[1152,256]{1,0:T(8,128)(2,1)} %param.17) | copy-start | bytes 1769476
  38.6 3.7 %copy-start.3 = (bf16[1152,256]{1,0:T(8,128)(2,1)S(1)}, bf16[1152,256]{1,0:T(8,128)(2,1)}, u32[]{:S(2)}) copy-start(bf16[1152,256]{1,0:T(8,128)(2,1)} %param.18) | copy-start | bytes 1769476
  39.3 0.6 copy-start.7
  39.3 3.3 %copy-start.4 = (bf16[1152,256]{1,0:T(8,128)(2,1)S(1)}, bf16[1152,256]{1,0:T(8,128)(2,1)}, u32[]{:S(2)}) copy-start(bf16[1152,256]{1,0:T(8,128)(2,1)} %param.19) | copy-start | bytes 1769476
  40.2 0.7 copy-start.5
  41.7 1.3 copy-start.6
  42.5 3.4 %copy-start.10 = (f32[256]{0:T(256)S(1)}, f32[256]{0:T(256)}, u32[]{:S(2)}) copy-start(f32[256]{0:T(256)} %param.24) | copy-start | bytes 3076
  42.6 3.3 %copy-start.8 = (bf16[128,256]{1,0:T(8,128)(2,1)S(1)}, bf16[128,256]{1,0:T(8,128)(2,1)}, u32[]{:S(2)}) copy-start(bf16[128,256]{1,0:T(8,128)(2,1)} %copy-done.7) | copy-start | bytes 196612
  47.1 38.7 %all-to-all-start.1 = ((bf16[128,8,128]{2,1,0:T(8,128)(2,1)}), bf16[128,8,128]{2,1,0:T(8,128)(2,1)S(1)}, u32[]{:S(2)}, u32[]{:S(2)}) async-start(bf16[128,8,128]{2,1,0:T(8,128)(2,1)} %copy.119), calls=%async_computation.1 | async-start | bytes 524288 | tf_op jit(solution)/shard_map/all_to_all | solution.py:157
  62.2 119.1 %all-gather.5.cloned.1.call-start = ((), (), s32[]{:S(2)}) async-start(), calls=%async_computation.7 | async-start | bytes 2820096 | tf_op jit(solution)/shard_map/all_gather | solution.py:129
  86.4 2.3 %copy-start.11 = (f32[256]{0:T(256)S(1)}, f32[256]{0:T(256)}, u32[]{:S(2)}) copy-start(f32[256]{0:T(256)} %param.25) | copy-start | bytes 3076
  87.9 37.0 %copy-start.1 = (bf16[1,1,32,1152]{3,2,1,0:T(8,128)(2,1)S(1)}, bf16[1,1,32,1152]{3,2,1,0:T(8,128)(2,1)}, u32[]{:S(2)}) copy-start(bf16[1,1,32,1152]{3,2,1,0:T(8,128)(2,1)} %param.15) | copy-start | bytes 221188
  88.0 37.3 %copy-start.14 = (f32[1152]{0:T(1024)S(1)}, f32[1152]{0:T(1024)}, u32[]{:S(2)}) copy-start(f32[1152]{0:T(1024)} %param.27) | copy-start | bytes 13828
  111.6 13.3 %all-to-all-start.3 = ((bf16[4,32,1152]{2,1,0:T(8,128)(2,1)}), bf16[4,32,1152]{2,1,0:T(8,128)(2,1)S(1)}, u32[]{:S(2)}, u32[]{:S(2)}) async-start(bf16[4,32,1152]{2,1,0:T(8,128)(2,1)} %bitcast.54), calls=%async_computation.3 | async-start | bytes 589824 | tf_op jit(solution)/shard_map/all_to_all | solution.py:26
Sparse Core Ops, SparseCore 0:
  34.0 74.0 all-gather.2
  110.2 71.0 all-gather.4
